TPU v7x, 32 devices: a whole 2x2x4 slice. The times are simulated.
32 devices in a mesh: rows: 4 (over y, core), cols: 8 (over z, x).
Axes of the slice: x: 2, y: 2, z: 4, core: 2. Of those that a mesh axis runs over, the one named last changes fastest.
Arguments:
- single: bfloat16 [512, 1024], P('rows'), may hold values from -6 to 6
- pair: bfloat16 [512, 512, 128], P('rows', 'cols'), may hold values from -6 to 6
- residue_mask: int32 [512], replicated, may hold values from 0 to 1, as said below
- w_bias: bfloat16 [128, 32], replicated, may hold values from -40 to 40
- w_project: bfloat16 [4, 1024, 1024], P(None, None, 'cols'), may hold values from -0.1875 to 0.1875
- w_out: bfloat16 [1024, 1024], replicated, may hold values from -0.1875 to 0.1875
- w_factors: bfloat16 [1024, 128], replicated, may hold values from -0.1875 to 0.1875
- w_pairout: bfloat16 [128, 128], replicated, may hold values from -0.5 to 0.5
- w_up: bfloat16 [128, 512], replicated, may hold values from -0.5 to 0.5
- w_down: bfloat16 [512, 128], replicated, may hold values from -0.25 to 0.25
Outputs:
- single_out: bfloat16 [512, 1024], P('rows')
- pair_out: bfloat16 [512, 512, 128], P('rows', 'cols')
Inputs may be any that keep to these rules, and one draw needn't show every extreme that they name: residue_mask is 1 on a leading run of at least 256 positions and 0 after it.
All inputs are finite; a program needn't handle non-finite values.
Results may differ from a plain program's by a relative error of at most 0.01.
The roundings to bfloat16 on the way count: a program that leaves them out, or rounds other values in their place, can miss the bound.
Values may be sent and summed in bfloat16 or wider, within the bound.
A program may use at most 64 MiB of HBM per device.

v0:
```python
import math
import jax
import jax.numpy as jnp
from jax import lax
from jax.sharding import PartitionSpec as P

epsilon = 1e-05


def from_root(value, axis, root):
    mine = lax.axis_index(axis) == root
    return lax.psum(jnp.where(mine, value, jnp.zeros_like(value)), axis)


def layer_norm(values):
    values = values.astype(jnp.float32)
    centred = values - jnp.mean(values, -1, keepdims=True)
    return centred * lax.rsqrt(jnp.mean(centred * centred, -1, keepdims=True) + epsilon)


def per_device(
    single, pair, residue_mask, w_bias, w_project, w_out, w_factors, w_pairout, w_up, w_down
):
    tile_rows = pair.shape[0]
    tile_cols = pair.shape[1]
    normed_pair = layer_norm(pair).astype(jnp.bfloat16)
    bias_local = jnp.einsum(
        "rcp,ph->hrc", normed_pair, w_bias, preferred_element_type=jnp.float32
    ).astype(jnp.bfloat16)
    normed_single = layer_norm(single).astype(jnp.bfloat16)
    projected = jnp.einsum(
        "rs,fsc->frc", normed_single, w_project, preferred_element_type=jnp.float32
    )
    query_rows = projected[0].astype(jnp.bfloat16)
    key_local = projected[1].astype(jnp.bfloat16)
    value_local = projected[2].astype(jnp.bfloat16)
    gate_values = jax.nn.sigmoid(projected[3])
    first_residue = lax.axis_index("cols") * tile_cols
    owner_row = first_residue // tile_rows
    offset_rows = first_residue - owner_row * tile_rows
    bias_heads = lax.all_to_all(bias_local, "cols", split_axis=0, concat_axis=2, tiled=True)
    key_rows, value_rows = (
        lax.all_gather(key_local, "rows", axis=0, tiled=True),
        lax.all_gather(value_local, "rows", axis=0, tiled=True),
    )
    heads_here = bias_heads.shape[0]
    head_width = query_rows.shape[1] // heads_here
    residues = key_rows.shape[0]
    query_split = query_rows.reshape(tile_rows, heads_here, head_width)
    key_split = key_rows.reshape(residues, heads_here, head_width)
    value_split = value_rows.reshape(residues, heads_here, head_width)
    score_scale = 1.0 / math.sqrt(head_width)
    scores = jnp.einsum(
        "rhd,lhd->hrl", query_split, key_split, preferred_element_type=jnp.float32
    ) * score_scale + bias_heads.astype(jnp.float32)
    key_valid = (residue_mask > 0)[None, None, :]
    scores = jnp.where(key_valid, scores, -jnp.inf)
    weights = jax.nn.softmax(scores, axis=-1).astype(jnp.bfloat16)
    attended = jnp.einsum("hrl,lhd->rhd", weights, value_split, preferred_element_type=jnp.float32)
    attended = attended.reshape(tile_rows, heads_here * head_width)
    mixed = (attended * gate_values).astype(jnp.bfloat16)
    whole_heads = lax.all_gather(mixed, "cols", axis=1, tiled=True)
    head_total = jnp.dot(whole_heads, w_out, preferred_element_type=jnp.float32)
    single_out = (single.astype(jnp.float32) + head_total).astype(jnp.bfloat16)
    normed_out = layer_norm(single_out).astype(jnp.bfloat16)
    factors = jnp.dot(normed_out, w_factors, preferred_element_type=jnp.float32).astype(
        jnp.bfloat16
    )
    factor_width = factors.shape[1] // 2
    left_factor = factors[:, :factor_width]
    right_local = factors[:, factor_width:]
    right_piece = lax.dynamic_slice_in_dim(right_local, offset_rows, tile_cols, 0)
    right_cols = from_root(right_piece, "rows", owner_row)
    block_rows = math.gcd(tile_rows, max(1, 4096 // tile_cols))
    count_blocks = tile_rows // block_rows

    def update_block(operands):
        pair_block, left_block = operands
        left_wide = left_block.astype(jnp.float32)[:, None, :]
        right_wide = right_cols.astype(jnp.float32)[None, :, :]
        paired = jnp.concatenate([left_wide * right_wide, left_wide - right_wide], -1).astype(
            jnp.bfloat16
        )
        pair_mid = (
            pair_block.astype(jnp.float32)
            + jnp.einsum("rcq,qp->rcp", paired, w_pairout, preferred_element_type=jnp.float32)
        ).astype(jnp.bfloat16)
        normed_mid = layer_norm(pair_mid).astype(jnp.bfloat16)
        hidden = jax.nn.relu(
            jnp.einsum("rcp,pk->rck", normed_mid, w_up, preferred_element_type=jnp.float32)
        ).astype(jnp.bfloat16)
        return (
            pair_mid.astype(jnp.float32)
            + jnp.einsum("rck,kp->rcp", hidden, w_down, preferred_element_type=jnp.float32)
        ).astype(jnp.bfloat16)

    updated = lax.map(
        update_block,
        (
            pair.reshape(count_blocks, block_rows, tile_cols, pair.shape[2]),
            left_factor.reshape(count_blocks, block_rows, factor_width),
        ),
    )
    return (single_out, updated.reshape(pair.shape))


def solution(mesh):
    return jax.shard_map(
        per_device,
        mesh=mesh,
        in_specs=(
            P("rows", None),
            P("rows", "cols", None),
            P(),
            P(),
            P(None, None, "cols"),
            P(),
            P(),
            P(),
            P(),
            P(),
        ),
        out_specs=(P("rows", None), P("rows", "cols", None)),
        check_vma=False,
    )
```

profile of v0, /device:TPU:0, one launch (start us, length us, event | category | flops | bytes accessed | tf_op | source)
XLA Modules:
  0.0 100.3 jit_solution(4183967973226425376)
XLA Ops:
  0.7 2.9 %convert_reduce_fusion.1 = f32[128,64]{1,0:T(8,128)S(1)} fusion(bf16[128,64,128]{2,1,0:T(8,128)(2,1)} %param.13), kind=kLoop, calls=%fused_computation.33 | loop fusion | flops 2088960 | bytes 2129920 | tf_op jit(solution)/shard_map/reduce_sum | solution.py:17
  3.6 2.7 %fusion.30 = f32[128,64]{1,0:T(8,128)S(1)} fusion(bf16[128,64,128]{2,1,0:T(8,128)(2,1)S(1)} %copy-done.1, f32[128,64]{1,0:T(8,128)S(1)} %broadcast_multiply_fusion.1), kind=kLoop, calls=%fused_computation.36 | loop fusion | flops 4186112 | bytes 2162688 | tf_op jit(solution)/shard_map/reduce_sum | solution.py:18
  6.4 3.4 %fusion.31 = bf16[128,64,128]{2,1,0:T(8,128)(2,1)S(1)} fusion(bf16[128,64,128]{2,1,0:T(8,128)(2,1)S(1)} %copy-done.1, f32[128,64]{1,0:T(8,128)S(1)} %add_rsqrt_fusion.1, f32[128,64]{1,0:T(8,128)S(1)} %broadcast_multiply_fusion.1), kind=kLoop, calls=%fused_computation.37 | loop fusion | flops 4194304 | bytes 4259840 | tf_op jit(solution)/shard_map/convert_element_type | solution.py:26
  9.8 1.4 %fusion.41 = bf16[32,128,64]{1,0,2:T(8,128)(2,1)S(1)} fusion(bf16[128,64,128]{2,1,0:T(8,128)(2,1)S(1)} %fusion.31, bf16[128,32]{0,1:T(8,128)(2,1)S(1)} %copy-done.7), kind=kOutput, calls=%fused_computation.46 | convolution fusion | flops 67371008 | bytes 2629632 | tf_op jit(solution)/shard_map/rcp,ph->hrc/dot_general | solution.py:27
  11.1 1.0 %copy.31 = bf16[32,128,64]{1,2,0:T(8,128)(2,1)} copy(bf16[32,128,64]{1,0,2:T(8,128)(2,1)S(1)} %fusion.41) | data formatting | bytes 1048576 | tf_op jit(solution)/shard_map/convert_element_type | solution.py:29
  12.2 7.3 %all-to-all-start = ((bf16[32,128,64]{1,2,0:T(8,128)(2,1)}), bf16[32,128,64]{1,2,0:T(8,128)(2,1)}, u32[]{:S(2)}, u32[]{:S(2)}) async-start(bf16[32,128,64]{1,2,0:T(8,128)(2,1)} %copy.31), calls=%async_computation | async-start | bytes 1048576 | tf_op jit(solution)/shard_map/all_to_all | solution.py:41
  19.9 1.5 %copy.29 = bf16[4,1024,128]{1,2,0:T(8,128)(2,1)S(1)} copy(bf16[4,1024,128]{2,1,0:T(8,128)(2,1)} %param.16) | data formatting | bytes 2097152 | tf_op args[4]
  21.3 0.5 fusion.55
  21.9 0.7 copy-done.4
  22.6 0.6 fusion.69
  23.2 5.4 %all-gather.1 = bf16[1,512,128]{1,2,0:T(8,128)(2,1)S(1)} all-gather(bf16[1,128,128]{1,2,0:T(8,128)(2,1)S(1)} %get-tuple-element.97), channel_id=3, replica_groups=mesh['rows'=4,'cols'=8] {'rows'}, dimensions={1}, use_global_device_ids=true | all-gather | bytes 163840 | tf_op jit(solution)/shard_map/all_gather | solution.py:43
  28.7 5.9 %all-gather = bf16[1,512,128]{1,2,0:T(8,128)(2,1)} all-gather(bf16[1,128,128]{1,2,0:T(8,128)(2,1)S(1)} %get-tuple-element.99), channel_id=2, replica_groups=mesh['rows'=4,'cols'=8] {'rows'}, dimensions={1}, use_global_device_ids=true | all-gather | bytes 163840 | tf_op jit(solution)/shard_map/all_gather | solution.py:44
  34.5 1.1 %convert_bitcast_fusion = f32[4,128,8,64]{1,3,0,2:T(8,128)S(1)} fusion(bf16[8,4,128,64]{2,3,1,0:T(8,128)(2,1)} %bitcast.28), kind=kLoop, calls=%fused_computation.50 | loop fusion | flops 262144 | bytes 1572864 | tf_op jit(solution)/shard_map/convert_element_type | solution.py:55
  35.8 1.3 %copy.33 = f32[4,128,512]{2,1,0:T(8,128)} copy(f32[4,128,512]{1,2,0:T(8,128)S(1)} %bitcast.77) | data formatting | bytes 2097152 | tf_op jit(solution)/shard_map/convert_element_type | solution.py:55
  37.1 1.6 %fusion.37 = f32[4,128,512]{2,1,0:T(8,128)S(1)} fusion(f32[4,128,512]{2,1,0:T(8,128)} %copy.33, bf16[128,4,32]{0,2,1:T(8,128)(2,1)} %bitcast.82, bf16[512,4,32]{0,2,1:T(8,128)(2,1)S(1)} %bitcast.80, pred[512]{0:T(512)(128)(4,1)S(1)} %broadcast_compare_fusion), kind=kOutput, calls=%fused_computation.44 | convolution fusion | flops 17563648 | bytes 2261504 | tf_op jit(solution)/shard_map/rhd,lhd->hrl/dot_general | solution.py:53
  39.0 1.9 %fusion.53 = f32[4,32,128]{2,1,0:T(8,128)S(1)} fusion(bf16[512,4,32]{0,2,1:T(8,128)(2,1)} %bitcast.83, f32[4,128]{1,0:T(4,128)S(1)} %fusion.71, f32[4,128,512]{2,1,0:T(8,128)S(1)} %fusion.37), kind=kOutput, calls=%fused_computation.64 | convolution fusion | flops 17564672 | bytes 1247232 | tf_op jit(solution)/shard_map/hrl,lhd->rhd/dot_general | solution.py:59
  41.0 0.9 fusion.66
  41.9 31.5 %all_gather.11 = bf16[128,1024]{0,1:T(8,128)(2,1)S(1)} all-gather(bf16[128,128]{0,1:T(8,128)(2,1)S(1)} %fusion.66), channel_id=1, replica_groups=mesh['rows'=4,'cols'=8] {'cols'}, dimensions={1}, use_global_device_ids=true | all-gather | bytes 294912 | tf_op jit(solution)/shard_map/all_gather | solution.py:62
  73.4 0.5 convert_reduce_fusion.3
  74.2 0.3 convolution_convert_fusion
  74.7 10.3 %psum.7 = bf16[64,64]{0,1:T(8,128)(2,1)S(1)} all-reduce(bf16[64,64]{0,1:T(8,128)(2,1)S(1)} %dynamic-slice_select_fusion), channel_id=1, replica_groups=mesh['rows'=4,'cols'=8] {'rows'}, use_global_device_ids=true, to_apply=%region_8.9 | all-reduce | flops 4096 | bytes 16384 | tf_op jit(solution)/shard_map/psum | solution.py:12
  85.2 15.0 %while.10 = (s32[]{:T(128)}, bf16[2,64,64,128]{3,2,1,0:T(8,128)(2,1)}, bf16[2,64,64,128]{3,2,1,0:T(8,128)(2,1)}, bf16[2,64,64]{2,1,0:T(8,128)(2,1)S(1)}, bf16[64...) while((s32[]{:T(128)}, ...), condition=%wide.region_12.13_spmd, body=%wide.region_9.12_spmd.sunk | while | flops 1223700480 | bytes 17334912 | solution.py:97
  85.3 0.5 multiply_convert_fusion.2
  85.8 1.0 copy-done.2
  86.8 1.2 %convert_reduce_fusion.5 = (f32[64,64]{1,0:T(8,128)S(1)}, bf16[64,64,128]{2,1,0:T(8,128)(2,1)S(1)}) fusion(bf16[128,128]{1,0:T(8,128)(2,1)S(1)} %get-tuple-element.184, bf16[64,64,64]{2,1,0:T(8,128)(2,1)S(1)} %get-tuple-element.157, bf16[64,64,64]{2,1,0:T(8,128)(2,1)S(1)} %get-tuple-element.158, bf16[2,64,64,128]{3,2,1,0:T(8,128)(2,1)S(1)} %copy-done.2, ...), kind=kOutput, calls=%fused_computation.6.clone.1 | convolution fusion | flops 138932224 | bytes 3194884 | tf_op jit(solution)/shard_map/while/body/eval_jaxpr/rcq,qp->rcp/dot_general | solution.py:86
  88.1 1.3 %fusion.89 = f32[64,64]{1,0:T(8,128)S(1)} fusion(bf16[64,64,128]{2,1,0:T(8,128)(2,1)S(1)} %get-tuple-element.159, f32[64,64]{1,0:T(8,128)S(1)} %broadcast_multiply_fusion.5), kind=kLoop, calls=%fused_computation.9.clone.1 | loop fusion | flops 2093056 | bytes 1081344 | tf_op jit(solution)/shard_map/while/body/eval_jaxpr/reduce_sum | solution.py:18
  89.4 3.4 %fusion.90 = bf16[2,64,64,128]{3,2,1,0:T(8,128)(2,1)} fusion(bf16[2,64,64,128]{3,2,1,0:T(8,128)(2,1)} %get-tuple-element.171, s32[]{:T(128)} %get-tuple-element.170, bf16[64,64,128]{2,1,0:T(8,128)(2,1)S(1)} %get-tuple-element.159, f32[64,64]{1,0:T(8,128)S(1)} %add_rsqrt_fusion.5, f32[64,64]{1,0:T(8,128)S(1)} %broadcast_multiply_fusion.5, ...), kind=kOutput, calls=%fused_computation.17.clone.1 | convolution fusion | flops 1081606144 | bytes 3473920 | tf_op jit(solution)/shard_map/while/body/eval_jaxpr/rck,kp->rcp/dot_general | solution.py:94
  92.8 0.5 multiply_convert_fusion.2
  93.3 1.0 %copy-done.2 = bf16[2,64,64,128]{3,2,1,0:T(8,128)(2,1)S(1)} copy-done((bf16[2,64,64,128]{3,2,1,0:T(8,128)(2,1)S(1)}, bf16[2,64,64,128]{3,2,1,0:T(8,128)(2,1)}, u32[]{:S(2)}) %copy-start.2) | copy-done | bytes 2097176 | tf_op jit(solution)/shard_map/while
  94.4 1.2 %convert_reduce_fusion.5 = (f32[64,64]{1,0:T(8,128)S(1)}, bf16[64,64,128]{2,1,0:T(8,128)(2,1)S(1)}) fusion(bf16[128,128]{1,0:T(8,128)(2,1)S(1)} %get-tuple-element.184, bf16[64,64,64]{2,1,0:T(8,128)(2,1)S(1)} %get-tuple-element.157, bf16[64,64,64]{2,1,0:T(8,128)(2,1)S(1)} %get-tuple-element.158, bf16[2,64,64,128]{3,2,1,0:T(8,128)(2,1)S(1)} %copy-done.2, ...), kind=kOutput, calls=%fused_computation.6.clone.1 | convolution fusion | flops 138932224 | bytes 3194884 | tf_op jit(solution)/shard_map/while/body/eval_jaxpr/rcq,qp->rcp/dot_general | solution.py:86
  95.6 1.3 %fusion.89 = f32[64,64]{1,0:T(8,128)S(1)} fusion(bf16[64,64,128]{2,1,0:T(8,128)(2,1)S(1)} %get-tuple-element.159, f32[64,64]{1,0:T(8,128)S(1)} %broadcast_multiply_fusion.5), kind=kLoop, calls=%fused_computation.9.clone.1 | loop fusion | flops 2093056 | bytes 1081344 | tf_op jit(solution)/shard_map/while/body/eval_jaxpr/reduce_sum | solution.py:18
  96.9 3.4 %fusion.90 = bf16[2,64,64,128]{3,2,1,0:T(8,128)(2,1)} fusion(bf16[2,64,64,128]{3,2,1,0:T(8,128)(2,1)} %get-tuple-element.171, s32[]{:T(128)} %get-tuple-element.170, bf16[64,64,128]{2,1,0:T(8,128)(2,1)S(1)} %get-tuple-element.159, f32[64,64]{1,0:T(8,128)S(1)} %add_rsqrt_fusion.5, f32[64,64]{1,0:T(8,128)S(1)} %broadcast_multiply_fusion.5, ...), kind=kOutput, calls=%fused_computation.17.clone.1 | convolution fusion | flops 1081606144 | bytes 3473920 | tf_op jit(solution)/shard_map/while/body/eval_jaxpr/rck,kp->rcp/dot_general | solution.py:94
  (50 shorter events, 1.4 us)
Async XLA Ops:
  0.6 72.8 %copy-start = (bf16[1024,1024]{1,0:T(8,128)(2,1)S(1)}, bf16[1024,1024]{1,0:T(8,128)(2,1)}, u32[]{:S(2)}) copy-start(bf16[1024,1024]{1,0:T(8,128)(2,1)} %param.17) | copy-start | bytes 6291460
  0.6 2.9 %copy-start.1 = (bf16[128,64,128]{2,1,0:T(8,128)(2,1)S(1)}, bf16[128,64,128]{2,1,0:T(8,128)(2,1)}, u32[]{:S(2)}) copy-start(bf16[128,64,128]{2,1,0:T(8,128)(2,1)} %param.13) | copy-start | bytes 6291460
  6.4 3.4 %copy-start.7 = (bf16[128,32]{0,1:T(8,128)(2,1)S(1)}, bf16[128,32]{0,1:T(8,128)(2,1)}, u32[]{:S(2)}) copy-start(bf16[128,32]{0,1:T(8,128)(2,1)} %param.15) | copy-start | bytes 24580
  9.7 9.7 %copy-start.3 = (bf16[128,1024]{1,0:T(8,128)(2,1)S(1)}, bf16[128,1024]{1,0:T(8,128)(2,1)}, u32[]{:S(2)}) copy-start(bf16[128,1024]{1,0:T(8,128)(2,1)} %param.12) | copy-start | bytes 786436
  12.2 22.4 %all-to-all-start = ((bf16[32,128,64]{1,2,0:T(8,128)(2,1)}), bf16[32,128,64]{1,2,0:T(8,128)(2,1)}, u32[]{:S(2)}, u32[]{:S(2)}) async-start(bf16[32,128,64]{1,2,0:T(8,128)(2,1)} %copy.31), calls=%async_computation | async-start | bytes 1048576 | tf_op jit(solution)/shard_map/all_to_all | solution.py:41
  19.8 14.7 %copy-start.8 = (s32[512]{0:T(512)S(1)}, s32[512]{0:T(512)}, u32[]{:S(2)}) copy-start(s32[512]{0:T(512)} %param.14) | copy-start | bytes 6148
  21.9 0.7 copy-start.4
  41.0 33.3 %copy-start.9 = (bf16[1024,128]{1,0:T(8,128)(2,1)S(1)}, bf16[1024,128]{1,0:T(8,128)(2,1)}, u32[]{:S(2)}) copy-start(bf16[1024,128]{1,0:T(8,128)(2,1)} %param.18) | copy-start | bytes 786436
  41.9 43.3 %copy-start.6 = (bf16[128,128]{1,0:T(8,128)(2,1)S(1)}, bf16[128,128]{1,0:T(8,128)(2,1)}, u32[]{:S(2)}) copy-start(bf16[128,128]{1,0:T(8,128)(2,1)} %param.19) | copy-start | bytes 98308
  41.9 43.3 %copy-start.10 = (bf16[128,512]{1,0:T(8,128)(2,1)S(1)}, bf16[128,512]{1,0:T(8,128)(2,1)}, u32[]{:S(2)}) copy-start(bf16[128,512]{1,0:T(8,128)(2,1)} %param.20) | copy-start | bytes 393220
  41.9 43.3 %copy-start.11 = (bf16[512,128]{1,0:T(8,128)(2,1)S(1)}, bf16[512,128]{1,0:T(8,128)(2,1)}, u32[]{:S(2)}) copy-start(bf16[512,128]{1,0:T(8,128)(2,1)} %param.21) | copy-start | bytes 393220
  74.0 11.2 %copy-start.5 = (bf16[128,1024]{1,0:T(8,128)(2,1)}, bf16[128,1024]{1,0:T(8,128)(2,1)S(1)}, u32[]{:S(2)}) copy-start(bf16[128,1024]{1,0:T(8,128)(2,1)S(1)} %get-tuple-element.103) | copy-start | bytes 786436
  85.2 1.6 %copy-start.2 = (bf16[2,64,64,128]{3,2,1,0:T(8,128)(2,1)S(1)}, bf16[2,64,64,128]{3,2,1,0:T(8,128)(2,1)}, u32[]{:S(2)}) copy-start(bf16[2,64,64,128]{3,2,1,0:T(8,128)(2,1)} %get-tuple-element.181) | copy-start | bytes 6291460 | tf_op jit(solution)/shard_map/while
  92.8 1.6 %copy-start.2 = (bf16[2,64,64,128]{3,2,1,0:T(8,128)(2,1)S(1)}, bf16[2,64,64,128]{3,2,1,0:T(8,128)(2,1)}, u32[]{:S(2)}) copy-start(bf16[2,64,64,128]{3,2,1,0:T(8,128)(2,1)} %get-tuple-element.181) | copy-start | bytes 6291460 | tf_op jit(solution)/shard_map/while
where the time goes:
time: 101 us; the launch traced here: 100 us
  blocking collectives  53.1 us (53%)
  other arithmetic  15.9 us (16%)
  matrix products  15.5 us (15%)
  local copies, waits for them, and re-layouts  7.51 us (7%)
  starting transfers between devices  7.28 us (7%)
    all_gather x1, blocking collectives, per_device(): whole_heads = lax.all_gather(mixed, 'cols', axis=1, tiled=True)  31.5 us
    psum x1, blocking collectives, from_root(): return lax.psum(jnp.where(mine, value, jnp.zeros_like(value)), axis)  10.3 us
    all_to_all x1, starting transfers between devices, per_device(): lax.all_to_all(bias_local, 'cols', split_axis=0, concat_axis=2, tiled=True)  7.28 us
    dot_general x2, matrix products, update_block(): jnp.einsum('rck,kp->rcp', hidden, w_down, preferred_element_type=jnp.floa...  6.75 us
    all_gather x1, blocking collectives, per_device(): lax.all_gather(value_local, 'rows', axis=0, tiled=True)  5.88 us
    reduce_sum x5, other arithmetic, layer_norm(): jnp.mean(centred * centred, -1, keepdims=True) + epsilon  5.77 us
    all_gather x1, blocking collectives, per_device(): lax.all_gather(key_local, 'rows', axis=0, tiled=True)  5.43 us
    convert_element_type x1, other arithmetic, per_device(): normed_pair = layer_norm(pair).astype(jnp.bfloat16)  3.36 us
  transfers between devices with their start and end apart: 1, of which 0 were waited for; matrix products, arithmetic and copies ran while one was open for 3% of the time, Pallas kernels for 0%

commit v1 on v0

--- a/solution.py
+++ b/solution.py
@@ -59,7 +59,12 @@
     attended = jnp.einsum("hrl,lhd->rhd", weights, value_split, preferred_element_type=jnp.float32)
     attended = attended.reshape(tile_rows, heads_here * head_width)
     mixed = (attended * gate_values).astype(jnp.bfloat16)
-    whole_heads = lax.all_gather(mixed, "cols", axis=1, tiled=True)
+    ring = [mixed]
+    for hop in range(7):
+        ring.append(lax.ppermute(ring[-1], "cols", [(dev, (dev + 1) % 8) for dev in range(8)]))
+    whole_heads = jnp.roll(
+        jnp.concatenate(ring[::-1], axis=1), (lax.axis_index("cols") + 1) * ring[0].shape[1], axis=1
+    )
     head_total = jnp.dot(whole_heads, w_out, preferred_element_type=jnp.float32)
     single_out = (single.astype(jnp.float32) + head_total).astype(jnp.bfloat16)
     normed_out = layer_norm(single_out).astype(jnp.bfloat16)

time: 101 us -> 118 us (1.17)
  waiting for transfers between devices: 0.01 us -> 44.3 us
  blocking collectives: 53.1 us -> 21.6 us
  starting transfers between devices: 7.28 us -> 9.37 us
  matrix products: 15.5 us -> 17.4 us
    ppermute x0 -> x7, waiting for transfers between devices: none -> 44.3 us  [per_device(): lax.ppermute(ring[-1], 'cols', [(dev, (dev + 1) % 8) for dev in range(8)])]
    all_gather x1 -> x0, blocking collectives: 31.5 us -> none  [per_device(): whole_heads = lax.all_gather(mixed, 'cols', axis=1, tiled=True)]
    ppermute x0 -> x7, starting transfers between devices: none -> 2.09 us  [per_device(): lax.ppermute(ring[-1], 'cols', [(dev, (dev + 1) % 8) for dev in range(8)])]
    dot_general x2, matrix products: 6.75 us -> 8.68 us  [update_block(): jnp.einsum('rck,kp->rcp', hidden, w_down, preferred_element_type=jnp.floa...]
    unnamed x23 -> x34, local copies, waits for them, and re-layouts: 2.25 us -> 2.85 us
  transfers between devices with their start and end apart: 1 -> 8, of which waited for: 0 -> 7; matrix products, arithmetic and copies ran while one was open for 3% -> 3% of each run, Pallas kernels for 0% -> 0%
where the time goes in v1:
time: 118 us
  waiting for transfers between devices  44.3 us (38%)
  blocking collectives  21.6 us (18%)
  matrix products  17.4 us (15%)
  other arithmetic  15.8 us (13%)
  starting transfers between devices  9.37 us (8%)
  local copies, waits for them, and re-layouts  8.09 us (7%)
    ppermute x7, waiting for transfers between devices, per_device(): lax.ppermute(ring[-1], 'cols', [(dev, (dev + 1) % 8) for dev in range(8)])  44.3 us
    psum x1, blocking collectives, from_root(): return lax.psum(jnp.where(mine, value, jnp.zeros_like(value)), axis)  10.3 us
    dot_general x2, matrix products, update_block(): jnp.einsum('rck,kp->rcp', hidden, w_down, preferred_element_type=jnp.floa...  8.68 us
    all_to_all x1, starting transfers between devices, per_device(): lax.all_to_all(bias_local, 'cols', split_axis=0, concat_axis=2, tiled=True)  7.28 us
    all_gather x1, blocking collectives, per_device(): lax.all_gather(value_local, 'rows', axis=0, tiled=True)  5.88 us
    reduce_sum x5, other arithmetic, layer_norm(): jnp.mean(centred * centred, -1, keepdims=True) + epsilon  5.77 us
    all_gather x1, blocking collectives, per_device(): lax.all_gather(key_local, 'rows', axis=0, tiled=True)  5.43 us
    convert_element_type x1, other arithmetic, per_device(): normed_pair = layer_norm(pair).astype(jnp.bfloat16)  3.36 us
  transfers between devices with their start and end apart: 8, of which 7 were waited for; matrix products, arithmetic and copies ran while one was open for 3% of the time, Pallas kernels for 0%

profile of v1, /device:TPU:0, one launch (start us, length us, event | category | flops | bytes accessed | tf_op | source)
XLA Modules:
  0.0 117.6 jit_solution(16938816608943584592)
XLA Ops:
  0.7 2.9 %convert_reduce_fusion.1 = f32[128,64]{1,0:T(8,128)S(1)} fusion(bf16[128,64,128]{2,1,0:T(8,128)(2,1)} %param.13), kind=kLoop, calls=%fused_computation.33 | loop fusion | flops 2088960 | bytes 2129920 | tf_op jit(solution)/shard_map/reduce_sum | solution.py:17
  3.6 2.7 %fusion.30 = f32[128,64]{1,0:T(8,128)S(1)} fusion(bf16[128,64,128]{2,1,0:T(8,128)(2,1)S(1)} %copy-done.1, f32[128,64]{1,0:T(8,128)S(1)} %broadcast_multiply_fusion.1), kind=kLoop, calls=%fused_computation.36 | loop fusion | flops 4186112 | bytes 2162688 | tf_op jit(solution)/shard_map/reduce_sum | solution.py:18
  6.4 3.4 %fusion.31 = bf16[128,64,128]{2,1,0:T(8,128)(2,1)S(1)} fusion(bf16[128,64,128]{2,1,0:T(8,128)(2,1)S(1)} %copy-done.1, f32[128,64]{1,0:T(8,128)S(1)} %add_rsqrt_fusion.1, f32[128,64]{1,0:T(8,128)S(1)} %broadcast_multiply_fusion.1), kind=kLoop, calls=%fused_computation.37 | loop fusion | flops 4194304 | bytes 4259840 | tf_op jit(solution)/shard_map/convert_element_type | solution.py:26
  9.8 1.4 %fusion.41 = bf16[32,128,64]{1,0,2:T(8,128)(2,1)S(1)} fusion(bf16[128,64,128]{2,1,0:T(8,128)(2,1)S(1)} %fusion.31, bf16[128,32]{0,1:T(8,128)(2,1)S(1)} %copy-done.7), kind=kOutput, calls=%fused_computation.46 | convolution fusion | flops 67371008 | bytes 2629632 | tf_op jit(solution)/shard_map/rcp,ph->hrc/dot_general | solution.py:27
  11.1 1.0 copy.31
  12.1 7.3 %all-to-all-start = ((bf16[32,128,64]{1,2,0:T(8,128)(2,1)}), bf16[32,128,64]{1,2,0:T(8,128)(2,1)}, u32[]{:S(2)}, u32[]{:S(2)}) async-start(bf16[32,128,64]{1,2,0:T(8,128)(2,1)} %copy.31), calls=%async_computation | async-start | bytes 1048576 | tf_op jit(solution)/shard_map/all_to_all | solution.py:41
  19.8 1.5 %copy.29 = bf16[4,1024,128]{1,2,0:T(8,128)(2,1)S(1)} copy(bf16[4,1024,128]{2,1,0:T(8,128)(2,1)} %param.16) | data formatting | bytes 2097152 | tf_op args[4]
  23.2 5.4 %all-gather.1 = bf16[1,512,128]{1,2,0:T(8,128)(2,1)S(1)} all-gather(bf16[1,128,128]{1,2,0:T(8,128)(2,1)S(1)} %get-tuple-element.97), channel_id=3, replica_groups=mesh['rows'=4,'cols'=8] {'rows'}, dimensions={1}, use_global_device_ids=true | all-gather | bytes 163840 | tf_op jit(solution)/shard_map/all_gather | solution.py:43
  28.6 5.9 %all-gather = bf16[1,512,128]{1,2,0:T(8,128)(2,1)} all-gather(bf16[1,128,128]{1,2,0:T(8,128)(2,1)S(1)} %get-tuple-element.99), channel_id=2, replica_groups=mesh['rows'=4,'cols'=8] {'rows'}, dimensions={1}, use_global_device_ids=true | all-gather | bytes 163840 | tf_op jit(solution)/shard_map/all_gather | solution.py:44
  34.5 1.1 convert_bitcast_fusion
  35.7 1.3 %copy.33 = f32[4,128,512]{2,1,0:T(8,128)} copy(f32[4,128,512]{1,2,0:T(8,128)S(1)} %bitcast.76) | data formatting | bytes 2097152 | tf_op jit(solution)/shard_map/convert_element_type | solution.py:55
  37.0 1.6 %fusion.37 = f32[4,128,512]{2,1,0:T(8,128)S(1)} fusion(f32[4,128,512]{2,1,0:T(8,128)} %copy.33, bf16[128,4,32]{0,2,1:T(8,128)(2,1)} %bitcast.81, bf16[512,4,32]{0,2,1:T(8,128)(2,1)S(1)} %bitcast.79, pred[512]{0:T(512)(128)(4,1)S(1)} %broadcast_compare_fusion), kind=kOutput, calls=%fused_computation.44 | convolution fusion | flops 17563648 | bytes 2261504 | tf_op jit(solution)/shard_map/rhd,lhd->hrl/dot_general | solution.py:53
  38.9 1.9 %fusion.53 = f32[4,32,128]{2,1,0:T(8,128)S(1)} fusion(bf16[512,4,32]{0,2,1:T(8,128)(2,1)} %bitcast.82, f32[4,128]{1,0:T(4,128)S(1)} %fusion.73, f32[4,128,512]{2,1,0:T(8,128)S(1)} %fusion.37), kind=kOutput, calls=%fused_computation.64 | convolution fusion | flops 17564672 | bytes 1247232 | tf_op jit(solution)/shard_map/hrl,lhd->rhd/dot_general | solution.py:59
  40.9 0.9 fusion.67
  41.8 2.1 %collective-permute-start = (bf16[128,128]{0,1:T(8,128)(2,1)S(1)}, bf16[128,128]{0,1:T(8,128)(2,1)S(1)}, u32[]{:S(2)}, u32[]{:S(2)}) collective-permute-start(bf16[128,128]{0,1:T(8,128)(2,1)S(1)} %fusion.67), channel_id=1, source_target_pairs={{0,1},{1,2},{2,3},{3,4},{4,5},{5,6},{6,7},{7,0},{8,9},{9,10},{10,1... | collective-permute-start | bytes 98312 | tf_op jit(solution)/shard_map/ppermute | solution.py:64
  43.8 4.6 %collective-permute-done = bf16[128,128]{0,1:T(8,128)(2,1)S(1)} collective-permute-done((bf16[128,128]{0,1:T(8,128)(2,1)S(1)}, bf16[128,128]{0,1:T(8,128)(2,1)S(1)}, u32[]{:S(2)}, u32[]{:S(2)}) %collective-permute-start) | collective-permute-done | bytes 32800 | tf_op jit(solution)/shard_map/ppermute | solution.py:64
  48.5 6.6 %collective-permute-done.1 = bf16[128,128]{0,1:T(8,128)(2,1)S(1)} collective-permute-done((bf16[128,128]{0,1:T(8,128)(2,1)S(1)}, bf16[128,128]{0,1:T(8,128)(2,1)S(1)}, u32[]{:S(2)}, u32[]{:S(2)}) %collective-permute-start.1) | collective-permute-done | bytes 32800 | tf_op jit(solution)/shard_map/ppermute | solution.py:64
  55.1 6.6 %collective-permute-done.2 = bf16[128,128]{0,1:T(8,128)(2,1)S(1)} collective-permute-done((bf16[128,128]{0,1:T(8,128)(2,1)S(1)}, bf16[128,128]{0,1:T(8,128)(2,1)S(1)}, u32[]{:S(2)}, u32[]{:S(2)}) %collective-permute-start.2) | collective-permute-done | bytes 32800 | tf_op jit(solution)/shard_map/ppermute | solution.py:64
  61.7 6.6 %collective-permute-done.3 = bf16[128,128]{0,1:T(8,128)(2,1)S(1)} collective-permute-done((bf16[128,128]{0,1:T(8,128)(2,1)S(1)}, bf16[128,128]{0,1:T(8,128)(2,1)S(1)}, u32[]{:S(2)}, u32[]{:S(2)}) %collective-permute-start.3) | collective-permute-done | bytes 32800 | tf_op jit(solution)/shard_map/ppermute | solution.py:64
  68.3 6.6 %collective-permute-done.4 = bf16[128,128]{0,1:T(8,128)(2,1)S(1)} collective-permute-done((bf16[128,128]{0,1:T(8,128)(2,1)S(1)}, bf16[128,128]{0,1:T(8,128)(2,1)S(1)}, u32[]{:S(2)}, u32[]{:S(2)}) %collective-permute-start.4) | collective-permute-done | bytes 32800 | tf_op jit(solution)/shard_map/ppermute | solution.py:64
  74.9 6.6 %collective-permute-done.5 = bf16[128,128]{0,1:T(8,128)(2,1)S(1)} collective-permute-done((bf16[128,128]{0,1:T(8,128)(2,1)S(1)}, bf16[128,128]{0,1:T(8,128)(2,1)S(1)}, u32[]{:S(2)}, u32[]{:S(2)}) %collective-permute-start.5) | collective-permute-done | bytes 32800 | tf_op jit(solution)/shard_map/ppermute | solution.py:64
  81.5 6.6 %collective-permute-done.6 = bf16[128,128]{0,1:T(8,128)(2,1)S(1)} collective-permute-done((bf16[128,128]{0,1:T(8,128)(2,1)S(1)}, bf16[128,128]{0,1:T(8,128)(2,1)S(1)}, u32[]{:S(2)}, u32[]{:S(2)}) %collective-permute-start.6) | collective-permute-done | bytes 32800 | tf_op jit(solution)/shard_map/ppermute | solution.py:64
  90.1 10.3 %psum.7 = bf16[64,64]{0,1:T(8,128)(2,1)S(1)} all-reduce(bf16[64,64]{0,1:T(8,128)(2,1)S(1)} %dynamic-slice_select_fusion), channel_id=1, replica_groups=mesh['rows'=4,'cols'=8] {'rows'}, use_global_device_ids=true, to_apply=%region_8.9 | all-reduce | flops 4096 | bytes 16384 | tf_op jit(solution)/shard_map/psum | solution.py:12
  100.6 17.0 %while.10 = (s32[]{:T(128)}, bf16[2,64,64,128]{3,2,1,0:T(8,128)(2,1)}, bf16[2,64,64,128]{3,2,1,0:T(8,128)(2,1)}, bf16[2,64,64]{2,1,0:T(8,128)(2,1)S(1)}, bf16[64...) while((s32[]{:T(128)}, ...), condition=%wide.region_12.13_spmd, body=%wide.region_9.12_spmd.sunk | while | flops 1223700480 | bytes 17334912 | solution.py:102
  101.2 1.0 copy-done.2
  102.2 1.2 %convert_reduce_fusion.5 = (f32[64,64]{1,0:T(8,128)S(1)}, bf16[64,64,128]{2,1,0:T(8,128)(2,1)S(1)}) fusion(bf16[128,128]{1,0:T(8,128)(2,1)S(1)} %get-tuple-element.184, bf16[64,64,64]{2,1,0:T(8,128)(2,1)S(1)} %get-tuple-element.157, bf16[64,64,64]{2,1,0:T(8,128)(2,1)S(1)} %get-tuple-element.158, bf16[2,64,64,128]{3,2,1,0:T(8,128)(2,1)S(1)} %copy-done.2, ...), kind=kOutput, calls=%fused_computation.6.clone.1 | convolution fusion | flops 138932224 | bytes 3194884 | tf_op jit(solution)/shard_map/while/body/eval_jaxpr/rcq,qp->rcp/dot_general | solution.py:91
  103.4 1.3 %fusion.90 = f32[64,64]{1,0:T(8,128)S(1)} fusion(bf16[64,64,128]{2,1,0:T(8,128)(2,1)S(1)} %get-tuple-element.159, f32[64,64]{1,0:T(8,128)S(1)} %broadcast_multiply_fusion.5), kind=kLoop, calls=%fused_computation.9.clone.1 | loop fusion | flops 2093056 | bytes 1081344 | tf_op jit(solution)/shard_map/while/body/eval_jaxpr/reduce_sum | solution.py:18
  104.8 4.3 %fusion.91 = bf16[2,64,64,128]{3,2,1,0:T(8,128)(2,1)} fusion(bf16[2,64,64,128]{3,2,1,0:T(8,128)(2,1)} %get-tuple-element.171, s32[]{:T(128)} %get-tuple-element.170, bf16[64,64,128]{2,1,0:T(8,128)(2,1)S(1)} %get-tuple-element.159, f32[64,64]{1,0:T(8,128)S(1)} %add_rsqrt_fusion.5, f32[64,64]{1,0:T(8,128)S(1)} %broadcast_multiply_fusion.5, ...), kind=kOutput, calls=%fused_computation.17.clone.1 | convolution fusion | flops 1081606144 | bytes 3473920 | tf_op jit(solution)/shard_map/while/body/eval_jaxpr/rck,kp->rcp/dot_general | solution.py:99
  109.7 1.0 copy-done.2
  110.7 1.2 %convert_reduce_fusion.5 = (f32[64,64]{1,0:T(8,128)S(1)}, bf16[64,64,128]{2,1,0:T(8,128)(2,1)S(1)}) fusion(bf16[128,128]{1,0:T(8,128)(2,1)S(1)} %get-tuple-element.184, bf16[64,64,64]{2,1,0:T(8,128)(2,1)S(1)} %get-tuple-element.157, bf16[64,64,64]{2,1,0:T(8,128)(2,1)S(1)} %get-tuple-element.158, bf16[2,64,64,128]{3,2,1,0:T(8,128)(2,1)S(1)} %copy-done.2, ...), kind=kOutput, calls=%fused_computation.6.clone.1 | convolution fusion | flops 138932224 | bytes 3194884 | tf_op jit(solution)/shard_map/while/body/eval_jaxpr/rcq,qp->rcp/dot_general | solution.py:91
  111.9 1.3 %fusion.90 = f32[64,64]{1,0:T(8,128)S(1)} fusion(bf16[64,64,128]{2,1,0:T(8,128)(2,1)S(1)} %get-tuple-element.159, f32[64,64]{1,0:T(8,128)S(1)} %broadcast_multiply_fusion.5), kind=kLoop, calls=%fused_computation.9.clone.1 | loop fusion | flops 2093056 | bytes 1081344 | tf_op jit(solution)/shard_map/while/body/eval_jaxpr/reduce_sum | solution.py:18
  113.3 4.3 %fusion.91 = bf16[2,64,64,128]{3,2,1,0:T(8,128)(2,1)} fusion(bf16[2,64,64,128]{3,2,1,0:T(8,128)(2,1)} %get-tuple-element.171, s32[]{:T(128)} %get-tuple-element.170, bf16[64,64,128]{2,1,0:T(8,128)(2,1)S(1)} %get-tuple-element.159, f32[64,64]{1,0:T(8,128)S(1)} %add_rsqrt_fusion.5, f32[64,64]{1,0:T(8,128)S(1)} %broadcast_multiply_fusion.5, ...), kind=kOutput, calls=%fused_computation.17.clone.1 | convolution fusion | flops 1081606144 | bytes 3473920 | tf_op jit(solution)/shard_map/while/body/eval_jaxpr/rck,kp->rcp/dot_general | solution.py:99
  (75 shorter events, 5.9 us)
Async XLA Ops:
  0.6 87.8 %copy-start = (bf16[1024,1024]{1,0:T(8,128)(2,1)S(1)}, bf16[1024,1024]{1,0:T(8,128)(2,1)}, u32[]{:S(2)}) copy-start(bf16[1024,1024]{1,0:T(8,128)(2,1)} %param.17) | copy-start | bytes 6291460
  0.6 2.9 %copy-start.1 = (bf16[128,64,128]{2,1,0:T(8,128)(2,1)S(1)}, bf16[128,64,128]{2,1,0:T(8,128)(2,1)}, u32[]{:S(2)}) copy-start(bf16[128,64,128]{2,1,0:T(8,128)(2,1)} %param.13) | copy-start | bytes 6291460
  6.4 3.4 %copy-start.7 = (bf16[128,32]{0,1:T(8,128)(2,1)S(1)}, bf16[128,32]{0,1:T(8,128)(2,1)}, u32[]{:S(2)}) copy-start(bf16[128,32]{0,1:T(8,128)(2,1)} %param.15) | copy-start | bytes 24580
  9.7 9.7 %copy-start.3 = (bf16[128,1024]{1,0:T(8,128)(2,1)S(1)}, bf16[128,1024]{1,0:T(8,128)(2,1)}, u32[]{:S(2)}) copy-start(bf16[128,1024]{1,0:T(8,128)(2,1)} %param.12) | copy-start | bytes 786436
  12.1 22.3 %all-to-all-start = ((bf16[32,128,64]{1,2,0:T(8,128)(2,1)}), bf16[32,128,64]{1,2,0:T(8,128)(2,1)}, u32[]{:S(2)}, u32[]{:S(2)}) async-start(bf16[32,128,64]{1,2,0:T(8,128)(2,1)} %copy.31), calls=%async_computation | async-start | bytes 1048576 | tf_op jit(solution)/shard_map/all_to_all | solution.py:41
  19.8 14.7 %copy-start.8 = (s32[512]{0:T(512)S(1)}, s32[512]{0:T(512)}, u32[]{:S(2)}) copy-start(s32[512]{0:T(512)} %param.14) | copy-start | bytes 6148
  21.8 0.7 copy-start.4
  41.8 6.7 %collective-permute-start = (bf16[128,128]{0,1:T(8,128)(2,1)S(1)}, bf16[128,128]{0,1:T(8,128)(2,1)S(1)}, u32[]{:S(2)}, u32[]{:S(2)}) collective-permute-start(bf16[128,128]{0,1:T(8,128)(2,1)S(1)} %fusion.67), channel_id=1, source_target_pairs={{0,1},{1,2},{2,3},{3,4},{4,5},{5,6},{6,7},{7,0},{8,9},{9,10},{10,1... | collective-permute-start | bytes 98312 | tf_op jit(solution)/shard_map/ppermute | solution.py:64
  48.5 6.6 %collective-permute-start.1 = (bf16[128,128]{0,1:T(8,128)(2,1)S(1)}, bf16[128,128]{0,1:T(8,128)(2,1)S(1)}, u32[]{:S(2)}, u32[]{:S(2)}) collective-permute-start(bf16[128,128]{0,1:T(8,128)(2,1)S(1)} %collective-permute-done), channel_id=1, source_target_pairs={{0,1},{1,2},{2,3},{3,4},{4,5},{5,6},{6,7},{7,0},{8,9},{9,10},{10,1... | collective-permute-start | bytes 98312 | tf_op jit(solution)/shard_map/ppermute | solution.py:64
  55.1 6.6 %collective-permute-start.2 = (bf16[128,128]{0,1:T(8,128)(2,1)S(1)}, bf16[128,128]{0,1:T(8,128)(2,1)S(1)}, u32[]{:S(2)}, u32[]{:S(2)}) collective-permute-start(bf16[128,128]{0,1:T(8,128)(2,1)S(1)} %collective-permute-done.1), channel_id=1, source_target_pairs={{0,1},{1,2},{2,3},{3,4},{4,5},{5,6},{6,7},{7,0},{8,9},{9,10},{10,1... | collective-permute-start | bytes 98312 | tf_op jit(solution)/shard_map/ppermute | solution.py:64
  61.7 6.6 %collective-permute-start.3 = (bf16[128,128]{0,1:T(8,128)(2,1)S(1)}, bf16[128,128]{0,1:T(8,128)(2,1)S(1)}, u32[]{:S(2)}, u32[]{:S(2)}) collective-permute-start(bf16[128,128]{0,1:T(8,128)(2,1)S(1)} %collective-permute-done.2), channel_id=1, source_target_pairs={{0,1},{1,2},{2,3},{3,4},{4,5},{5,6},{6,7},{7,0},{8,9},{9,10},{10,1... | collective-permute-start | bytes 98312 | tf_op jit(solution)/shard_map/ppermute | solution.py:64
  68.3 6.6 %collective-permute-start.4 = (bf16[128,128]{0,1:T(8,128)(2,1)S(1)}, bf16[128,128]{0,1:T(8,128)(2,1)S(1)}, u32[]{:S(2)}, u32[]{:S(2)}) collective-permute-start(bf16[128,128]{0,1:T(8,128)(2,1)S(1)} %collective-permute-done.3), channel_id=1, source_target_pairs={{0,1},{1,2},{2,3},{3,4},{4,5},{5,6},{6,7},{7,0},{8,9},{9,10},{10,1... | collective-permute-start | bytes 98312 | tf_op jit(solution)/shard_map/ppermute | solution.py:64
  74.9 6.6 %collective-permute-start.5 = (bf16[128,128]{0,1:T(8,128)(2,1)S(1)}, bf16[128,128]{0,1:T(8,128)(2,1)S(1)}, u32[]{:S(2)}, u32[]{:S(2)}) collective-permute-start(bf16[128,128]{0,1:T(8,128)(2,1)S(1)} %collective-permute-done.4), channel_id=1, source_target_pairs={{0,1},{1,2},{2,3},{3,4},{4,5},{5,6},{6,7},{7,0},{8,9},{9,10},{10,1... | collective-permute-start | bytes 98312 | tf_op jit(solution)/shard_map/ppermute | solution.py:64
  81.5 6.6 %collective-permute-start.6 = (bf16[128,128]{0,1:T(8,128)(2,1)S(1)}, bf16[128,128]{0,1:T(8,128)(2,1)S(1)}, u32[]{:S(2)}, u32[]{:S(2)}) collective-permute-start(bf16[128,128]{0,1:T(8,128)(2,1)S(1)} %collective-permute-done.5), channel_id=1, source_target_pairs={{0,1},{1,2},{2,3},{3,4},{4,5},{5,6},{6,7},{7,0},{8,9},{9,10},{10,1... | collective-permute-start | bytes 98312 | tf_op jit(solution)/shard_map/ppermute | solution.py:64
  81.5 8.1 %copy-start.9 = (bf16[1024,128]{1,0:T(8,128)(2,1)S(1)}, bf16[1024,128]{1,0:T(8,128)(2,1)}, u32[]{:S(2)}) copy-start(bf16[1024,128]{1,0:T(8,128)(2,1)} %param.18) | copy-start | bytes 786436
  88.3 12.3 %copy-start.6 = (bf16[128,128]{1,0:T(8,128)(2,1)S(1)}, bf16[128,128]{1,0:T(8,128)(2,1)}, u32[]{:S(2)}) copy-start(bf16[128,128]{1,0:T(8,128)(2,1)} %param.19) | copy-start | bytes 98308
  89.0 0.7 copy-start.5
  100.6 1.6 %copy-start.2 = (bf16[2,64,64,128]{3,2,1,0:T(8,128)(2,1)S(1)}, bf16[2,64,64,128]{3,2,1,0:T(8,128)(2,1)}, u32[]{:S(2)}) copy-start(bf16[2,64,64,128]{3,2,1,0:T(8,128)(2,1)} %get-tuple-element.181) | copy-start | bytes 6291460 | tf_op jit(solution)/shard_map/while
  109.1 1.6 %copy-start.2 = (bf16[2,64,64,128]{3,2,1,0:T(8,128)(2,1)S(1)}, bf16[2,64,64,128]{3,2,1,0:T(8,128)(2,1)}, u32[]{:S(2)}) copy-start(bf16[2,64,64,128]{3,2,1,0:T(8,128)(2,1)} %get-tuple-element.181) | copy-start | bytes 6291460 | tf_op jit(solution)/shard_map/while
